TPU v7x, 32 devices: a whole 2x2x4 slice. The times are simulated.
32 devices in a mesh: member: 4 (over y, x), space: 8 (over z, core).
Axes of the slice: x: 2, y: 2, z: 4, core: 2. Of those that a mesh axis runs over, the one named last changes fastest.
Arguments:
- ensemble_prediction: bfloat16 [4, 300, 128, 128], P('member', None, 'space'), may hold values from -6 to 6
- observed_analysis: bfloat16 [300, 128, 128], P(None, 'space'), may hold values from -6 to 6
- validity_flags: int32 [2, 128, 128], P(None, 'space'), may hold values from 0 to 1, as said below
Outputs:
- point_score: float32 [300, 128, 128], P(None, 'space')
- channel_loss: float32 [300], replicated
Inputs may be any that keep to these rules, and one draw needn't show every extreme that they name: `validity_flags`: 0 or 1 for each point and group; every point of latitude row 11 is valid in both groups.
All inputs are finite; a program needn't handle non-finite values.
Results may differ from a plain program's by a relative error of at most 0.0003.
Values may be sent and summed in bfloat16 or wider, within the bound.
A program may use at most 64 MiB of HBM per device.

v0:
```python
import jax
import jax.numpy as jnp
from jax import lax
from jax.sharding import PartitionSpec as P

VARIABLE_NUMBER = 300
ATMOS = 180
TILE_SITES = 128
LON = 720
ROWS = 360


def per_channel(values):
    is_ocean = jnp.arange(VARIABLE_NUMBER, dtype=jnp.int32) >= ATMOS
    return jnp.where(is_ocean, values[1], values[0])


def shards(ensemble_prediction, observed_analysis, validity_flags):
    blocks_here = observed_analysis.shape[1]
    realization_entries = lax.axis_size("member")
    lat_rows = min(ROWS, blocks_here * lax.axis_size("space") * TILE_SITES // LON)
    first_point = lax.axis_index("space") * (blocks_here * TILE_SITES)
    position = first_point + jnp.arange(blocks_here * TILE_SITES, dtype=jnp.int32).reshape(
        blocks_here, TILE_SITES
    )
    inside = (position < lat_rows * LON).astype(jnp.float32)
    lat_row = (position // LON).astype(jnp.float32)
    cosine = jnp.cos(jnp.pi * ((lat_row + 0.5) / lat_rows - 0.5))
    valid = inside[None] * (validity_flags > 0).astype(jnp.float32)
    weight = cosine[None] * valid
    local_area = jnp.sum(weight, axis=(1, 2))
    local_count = jnp.sum(valid, axis=(1, 2))
    is_ocean = jnp.arange(VARIABLE_NUMBER, dtype=jnp.int32) >= ATMOS
    weight_chan = jnp.where(is_ocean[:, None, None], weight[1][None], weight[0][None])
    coeff = (1.0 - 0.05 / realization_entries) / (
        2.0 * realization_entries * (realization_entries - 1)
    )
    gathered = lax.all_to_all(
        ensemble_prediction, "member", split_axis=2, concat_axis=0, tiled=True
    )
    share = blocks_here // realization_entries
    first_block = lax.axis_index("member") * share
    target_part = lax.dynamic_slice_in_dim(observed_analysis, first_block, share, 1).astype(
        jnp.float32
    )
    accuracy_component = jnp.zeros(target_part.shape, jnp.float32)
    dispersion_component = jnp.zeros(target_part.shape, jnp.float32)
    for leading_realization in range(realization_entries):
        lead = gathered[leading_realization].astype(jnp.float32)
        accuracy_component = accuracy_component + jnp.abs(lead - target_part)
        for trailing_realization in range(leading_realization + 1, realization_entries):
            dispersion_component = dispersion_component + jnp.abs(
                lead - gathered[trailing_realization].astype(jnp.float32)
            )
    partial_crps = accuracy_component / realization_entries - coeff * (2.0 * dispersion_component)
    crps = lax.all_gather(partial_crps, "member", axis=1, tiled=True)
    area_sum, count = lax.psum((local_area, local_count), "space")
    scale_chan = per_channel(count / area_sum)
    point_score = crps * weight_chan * scale_chan[:, None, None]
    score_sums = lax.psum(jnp.sum(point_score, axis=(1, 2)), "space")
    channel_loss = score_sums / per_channel(count)
    return (point_score, channel_loss)


def solution(mesh):
    in_specs = (P("member", None, "space", None), P(None, "space", None), P(None, "space", None))
    out_specs = (P(None, "space", None), P())
    return jax.shard_map(shards, mesh=mesh, in_specs=in_specs, out_specs=out_specs, check_vma=False)
```

profile of v0, /device:TPU:0, one launch (start us, length us, event | category | flops | bytes accessed | tf_op | source)
XLA Modules:
  0.0 100.8 jit_solution(2808371847547564155)
XLA Ops:
  7.2 0.0 copy-start
  7.2 2.7 %copy.11 = bf16[1,300,16,128]{3,1,0,2:T(8,128)(2,1)} copy(bf16[1,300,16,128]{3,2,1,0:T(8,128)(2,1)} %param.3) | data formatting | bytes 2457600 | tf_op args[0]
  9.9 0.0 copy-start.1
  9.9 5.3 %all-to-all-start = ((bf16[1,300,16,128]{3,1,0,2:T(8,128)(2,1)}), bf16[1,300,16,128]{3,1,0,2:T(8,128)(2,1)S(1)}, u32[]{:S(2)}, u32[]{:S(2)}) async-start(bf16[1,300,16,128]{3,1,0,2:T(8,128)(2,1)} %copy.11), calls=%async_computation | async-start | bytes 2490368 | tf_op jit(solution)/shard_map/all_to_all | solution.py:38
  15.2 0.0 all-gather.2.cloned.1.call-start
  15.2 0.0 copy-done
  15.2 0.2 constant_dynamic-slice_fusion
  15.4 15.6 %all-to-all-done = bf16[1,300,16,128]{3,1,0,2:T(8,128)(2,1)S(1)} async-done(((bf16[1,300,16,128]{3,1,0,2:T(8,128)(2,1)}), bf16[1,300,16,128]{3,1,0,2:T(8,128)(2,1)S(1)}, u32[]{:S(2)}, u32[]{:S(2)}) %all-to-all-start) | async-done | bytes 1228832 | tf_op jit(solution)/shard_map/all_to_all | solution.py:38
  31.0 1.6 %fusion.5 = f32[300,4,128]{2,0,1:T(8,128)} fusion(bf16[4,1,300,4,128]{4,2,3,0,1:T(8,128)(2,1)S(1)} %bitcast.33, bf16[4,1,300,4,128]{4,2,3,1,0:T(8,128)(2,1)S(1)} %bitcast.34, bf16[300,4,128]{2,1,0:T(4,128)(2,1)S(1)} %constant_dynamic-slice_fusion), kind=kLoop, calls=%fused_computation.16 | loop fusion | flops 5529600 | bytes 2150400 | tf_op jit(solution)/shard_map/sub | solution.py:55
  32.5 0.0 all-gather.2.cloned.1.call-update
  32.6 0.1 fusion.26
  32.7 0.0 copy-done.1
  32.7 0.1 fusion.31
  32.8 0.1 select_reduce_fusion
  32.9 15.9 %all-reduce = (f32[2]{0:T(128)S(1)}, f32[2]{0:T(128)S(1)}) all-reduce(f32[2]{0:T(128)S(1)} %select_reduce_fusion, f32[2]{0:T(128)S(1)} %get-tuple-element.10), channel_id=1, replica_groups=mesh['member'=4,'space'=8] {'space'}, use_global_device_ids=true, to_apply=%region_1.2 | all-reduce | flops 4 | bytes 32 | tf_op jit(solution)/shard_map/psum | solution.py:57
  48.8 0.6 fusion.33
  49.4 1.3 %broadcast_select_fusion = f32[300]{0:T(512)S(1)} fusion(f32[]{:T(128)} %bitcast.16, f32[]{:T(128)} %bitcast.15), kind=kLoop, calls=%fused_computation.56 | loop fusion | flops 600 | bytes 1208 | tf_op jit(solution)/shard_map/jit(_where)/select_n | solution.py:15
  50.7 0.6 fusion.32
  51.3 20.2 %all-gather.2.cloned.1.call-done = f32[300,16,128]{2,0,1:T(8,128)} async-done(((f32[300,4,128]{2,0,1:T(8,128)}), f32[300,16,128]{2,0,1:T(8,128)}) %all-gather.2.cloned.1.call-update) | async-done | bytes 2457616 | tf_op jit(solution)/shard_map/all_gather | solution.py:56
  71.5 2.2 %fusion.30 = (f32[300]{0:T(512)S(1)}, f32[300,16,128]{2,0,1:T(8,128)S(1)}) fusion(f32[300]{0:T(512)S(1)} %broadcast_select_fusion, f32[300,16,128]{2,0,1:T(8,128)} %all-gather.2.cloned.1.call-done, f32[16,128]{1,0:T(8,128)S(1)} %get-tuple-element.14, f32[16,128]{1,0:T(8,128)S(1)} %get-tuple-element.13, pred[300]{0:T(512)(128)(4,1)S(1)} %iota_compare_fusion), kind=kLoop, calls=%fused_computation.58 | loop fusion | flops 2457300 | bytes 4934284 | tf_op jit(solution)/shard_map/reduce_sum | solution.py:60
  73.7 2.2 %copy.16 = f32[300,16,128]{2,1,0:T(8,128)} copy(f32[300,16,128]{2,0,1:T(8,128)S(1)} %get-tuple-element.9) | data formatting | bytes 4915200
  75.9 16.2 %psum.23 = f32[300]{0:T(512)S(1)} all-reduce(f32[300]{0:T(512)S(1)} %get-tuple-element.8), channel_id=1, replica_groups=mesh['member'=4,'space'=8] {'space'}, use_global_device_ids=true, to_apply=%region_5.6 | all-reduce | flops 300 | bytes 2400 | tf_op jit(solution)/shard_map/psum | solution.py:60
  92.1 1.9 %select_divide_fusion = f32[300]{0:T(512)} fusion(f32[300]{0:T(512)S(1)} %psum.23, f32[]{:T(128)} %bitcast.18, f32[]{:T(128)} %bitcast.17), kind=kLoop, calls=%fused_computation.54 | loop fusion | flops 900 | bytes 2408 | tf_op jit(solution)/shard_map/div | solution.py:61
  (4 shorter events, 0.0 us)
Async XLA Ops:
  7.2 8.1 %copy-start = (bf16[300,16,128]{2,1,0:T(8,128)(2,1)S(1)}, bf16[300,16,128]{2,1,0:T(8,128)(2,1)}, u32[]{:S(2)}) copy-start(bf16[300,16,128]{2,1,0:T(8,128)(2,1)} %param.4) | copy-start | bytes 3686404
  9.9 22.7 %copy-start.1 = (s32[2,16,128]{2,1,0:T(8,128)S(1)}, s32[2,16,128]{2,1,0:T(8,128)}, u32[]{:S(2)}) copy-start(s32[2,16,128]{2,1,0:T(8,128)} %param.5) | copy-start | bytes 49156
  9.9 21.1 %all-to-all-start = ((bf16[1,300,16,128]{3,1,0,2:T(8,128)(2,1)}), bf16[1,300,16,128]{3,1,0,2:T(8,128)(2,1)S(1)}, u32[]{:S(2)}, u32[]{:S(2)}) async-start(bf16[1,300,16,128]{3,1,0,2:T(8,128)(2,1)} %copy.11), calls=%async_computation | async-start | bytes 2490368 | tf_op jit(solution)/shard_map/all_to_all | solution.py:38
  15.2 56.2 %all-gather.2.cloned.1.call-start = ((), (), s32[]{:S(2)}) async-start(), calls=%async_computation.1 | async-start | bytes 3112960 | tf_op jit(solution)/shard_map/all_gather | solution.py:56
Sparse Core Ops, SparseCore 0:
  32.7 38.7 all-gather.1
where the time goes:
time: 101 us
  waiting for transfers between devices  35.8 us (35%)
  blocking collectives  32.1 us (32%)
  between operations  14.1 us (14%)
  other arithmetic  7.25 us (7%)
  local copies, waits for them, and re-layouts  6.33 us (6%)
  starting transfers between devices  5.33 us (5%)
    all_gather x1, waiting for transfers between devices, shards(): crps = lax.all_gather(partial_crps, 'member', axis=1, tiled=True)  20.2 us
    psum x1, blocking collectives, shards(): score_sums = lax.psum(jnp.sum(point_score, axis=(1, 2)), 'space')  16.2 us
    psum x1, blocking collectives, shards(): area_sum, count = lax.psum((local_area, local_count), 'space')  15.9 us
    all_to_all x1, waiting for transfers between devices, shards(): lax.all_to_all(ensemble_prediction, 'member', split_axis=2, concat_axis=0...  15.6 us
    all_to_all x1, starting transfers between devices, shards(): lax.all_to_all(ensemble_prediction, 'member', split_axis=2, concat_axis=0...  5.32 us
    unnamed x6, local copies, waits for them, and re-layouts  4.95 us
    reduce_sum x1, other arithmetic, shards(): score_sums = lax.psum(jnp.sum(point_score, axis=(1, 2)), 'space')  2.23 us
  transfers between devices with their start and end apart: 2, of which 2 were waited for; matrix products, arithmetic and copies ran while one was open for 3% of the time, Pallas kernels for 0%

commit v1 on v0

--- a/solution.py
+++ b/solution.py
@@ -8,6 +8,22 @@
 TILE_SITES = 128
 LON = 720
 ROWS = 360
+
+
+def skins_check(shard_in, join_dim):
+    width = lax.axis_size("member")
+    items = tuple(((j, (j + 1) % width) for j in range(width)))
+
+    def _expand_values(tmp):
+        if len(tmp) == width:
+            return tmp
+        return _expand_values([lax.ppermute(tmp[0], perm=items, axis_name="member"), *tmp])
+
+    return jnp.roll(
+        jnp.concatenate(_expand_values([shard_in]), axis=join_dim),
+        (lax.axis_index("member") + 1) * shard_in.shape[join_dim],
+        axis=join_dim,
+    )
 
 
 def per_channel(values):
@@ -53,7 +69,7 @@
                 lead - gathered[trailing_realization].astype(jnp.float32)
             )
     partial_crps = accuracy_component / realization_entries - coeff * (2.0 * dispersion_component)
-    crps = lax.all_gather(partial_crps, "member", axis=1, tiled=True)
+    crps = skins_check(partial_crps, 1)
     area_sum, count = lax.psum((local_area, local_count), "space")
     scale_chan = per_channel(count / area_sum)
     point_score = crps * weight_chan * scale_chan[:, None, None]

time: 101 us -> 93.8 us (0.929)
  between operations: 14.1 us -> 0.75 us
  waiting for transfers between devices: 35.8 us -> 44.3 us
  blocking collectives: 32.1 us -> 27.8 us
  local copies, waits for them, and re-layouts: 6.33 us -> 9.08 us
  other arithmetic: 7.25 us -> 4.68 us
  starting transfers between devices: 5.33 us -> 6.81 us
    ppermute x0 -> x3, waiting for transfers between devices: none -> 28.7 us  [_expand_values(): lax.ppermute(tmp[0], perm=items, axis_name='member')]
    all_gather x1 -> x0, waiting for transfers between devices: 20.2 us -> none  [shards(): crps = lax.all_gather(partial_crps, 'member', axis=1, tiled=True)]
    psum x1, blocking collectives: 16.2 us -> 13.6 us  [shards(): score_sums = lax.psum(jnp.sum(point_score, axis=(1, 2)), 'space')]
    unnamed x6 -> x13, local copies, waits for them, and re-layouts: 4.95 us -> 7.39 us
    psum x1, blocking collectives: 15.9 us -> 14.2 us  [shards(): area_sum, count = lax.psum((local_area, local_count), 'space')]
    reduce_sum x1, other arithmetic: 2.23 us -> 0.53 us  [shards(): score_sums = lax.psum(jnp.sum(point_score, axis=(1, 2)), 'space')]
    ppermute x0 -> x3, starting transfers between devices: none -> 1.62 us  [_expand_values(): lax.ppermute(tmp[0], perm=items, axis_name='member')]
  transfers between devices with their start and end apart: 2 -> 4, of which waited for: 2 -> 3; matrix products, arithmetic and copies ran while one was open for 3% -> 3% of each run, Pallas kernels for 0% -> 0%
where the time goes in v1:
time: 93.8 us; the launch traced here: 93.4 us
  waiting for transfers between devices  44.3 us (47%)
  blocking collectives  27.8 us (30%)
  local copies, waits for them, and re-layouts  9.08 us (10%)
  starting transfers between devices  6.81 us (7%)
  other arithmetic  4.68 us (5%)
    ppermute x3, waiting for transfers between devices, _expand_values(): lax.ppermute(tmp[0], perm=items, axis_name='member')  28.7 us
    all_to_all x1, waiting for transfers between devices, shards(): lax.all_to_all(ensemble_prediction, 'member', split_axis=2, concat_axis=0...  15.6 us
    psum x1, blocking collectives, shards(): area_sum, count = lax.psum((local_area, local_count), 'space')  14.2 us
    psum x1, blocking collectives, shards(): score_sums = lax.psum(jnp.sum(point_score, axis=(1, 2)), 'space')  13.6 us
    unnamed x13, local copies, waits for them, and re-layouts  7.39 us
    all_to_all x1, starting transfers between devices, shards(): lax.all_to_all(ensemble_prediction, 'member', split_axis=2, concat_axis=0...  5.19 us
  transfers between devices with their start and end apart: 4, of which 3 were waited for; matrix products, arithmetic and copies ran while one was open for 3% of the time, Pallas kernels for 0%

profile of v1, /device:TPU:0, one launch (start us, length us, event | category | flops | bytes accessed | tf_op | source)
XLA Modules:
  0.0 93.4 jit_solution(7731339194148546315)
XLA Ops:
  0.6 0.0 copy-start
  0.6 0.0 copy-start.1
  0.7 2.7 %copy.11 = bf16[1,300,16,128]{3,1,0,2:T(8,128)(2,1)} copy(bf16[1,300,16,128]{3,2,1,0:T(8,128)(2,1)} %param.3) | data formatting | bytes 2457600 | tf_op args[0]
  3.4 5.2 %all-to-all-start = ((bf16[1,300,16,128]{3,1,0,2:T(8,128)(2,1)}), bf16[1,300,16,128]{3,1,0,2:T(8,128)(2,1)S(1)}, u32[]{:S(2)}, u32[]{:S(2)}) async-start(bf16[1,300,16,128]{3,1,0,2:T(8,128)(2,1)} %copy.11), calls=%async_computation | async-start | bytes 2490368 | tf_op jit(solution)/shard_map/all_to_all | solution.py:54
  8.6 0.0 copy-done
  8.6 0.2 constant_dynamic-slice_fusion
  8.8 15.6 %all-to-all-done = bf16[1,300,16,128]{3,1,0,2:T(8,128)(2,1)S(1)} async-done(((bf16[1,300,16,128]{3,1,0,2:T(8,128)(2,1)}), bf16[1,300,16,128]{3,1,0,2:T(8,128)(2,1)S(1)}, u32[]{:S(2)}, u32[]{:S(2)}) %all-to-all-start) | async-done | bytes 1228832 | tf_op jit(solution)/shard_map/all_to_all | solution.py:54
  24.3 0.7 fusion.5
  25.1 0.2 copy.16
  25.3 1.5 %collective-permute-start = (f32[300,4,128]{2,1,0:T(4,128)S(1)}, f32[300,4,128]{2,1,0:T(4,128)S(1)}, u32[]{:S(2)}, u32[]{:S(2)}) collective-permute-start(f32[300,4,128]{2,1,0:T(4,128)S(1)} %copy.16), channel_id=1, source_target_pairs={{0,8},{8,16},{16,24},{24,0},{1,9},{9,17},{17,25},{25,1},{2,10},{10... | collective-permute-start | bytes 1843208 | tf_op jit(solution)/shard_map/ppermute | solution.py:20
  26.8 14.3 %collective-permute-done = f32[300,4,128]{2,1,0:T(4,128)S(1)} collective-permute-done((f32[300,4,128]{2,1,0:T(4,128)S(1)}, f32[300,4,128]{2,1,0:T(4,128)S(1)}, u32[]{:S(2)}, u32[]{:S(2)}) %collective-permute-start) | collective-permute-done | bytes 614432 | tf_op jit(solution)/shard_map/ppermute | solution.py:20
  41.1 0.1 collective-permute-start.1
  41.2 0.1 fusion.26
  41.3 0.0 copy-done.1
  41.3 0.1 fusion.31
  41.4 0.1 select_reduce_fusion
  41.5 14.4 %collective-permute-done.1 = f32[300,4,128]{2,1,0:T(4,128)S(1)} collective-permute-done((f32[300,4,128]{2,1,0:T(4,128)S(1)}, f32[300,4,128]{2,1,0:T(4,128)S(1)}, u32[]{:S(2)}, u32[]{:S(2)}) %collective-permute-start.1) | collective-permute-done | bytes 614432 | tf_op jit(solution)/shard_map/ppermute | solution.py:20
  56.0 0.0 collective-permute-start.2
  56.0 14.2 %all-reduce = (f32[2]{0:T(128)S(1)}, f32[2]{0:T(128)S(1)}) all-reduce(f32[2]{0:T(128)S(1)} %select_reduce_fusion, f32[2]{0:T(128)S(1)} %get-tuple-element.10), channel_id=1, replica_groups=mesh['member'=4,'space'=8] {'space'}, use_global_device_ids=true, to_apply=%region_1.2 | all-reduce | flops 4 | bytes 32 | tf_op jit(solution)/shard_map/psum | solution.py:73
  70.2 0.6 fusion.33
  70.8 1.3 %broadcast_select_fusion = f32[300]{0:T(512)S(1)} fusion(f32[]{:T(128)} %bitcast.16, f32[]{:T(128)} %bitcast.15), kind=kLoop, calls=%fused_computation.64 | loop fusion | flops 600 | bytes 1208 | tf_op jit(solution)/shard_map/jit(_where)/select_n | solution.py:31
  72.1 0.6 fusion.32
  72.7 0.0 collective-permute-done.2
  72.7 1.1 %copy_dynamic-update-slice_fusion.4 = f32[300,32,128]{2,0,1:T(8,128)S(1)} fusion(f32[300,4,128]{2,1,0:T(4,128)} %collective-permute-done.2), kind=kLoop, calls=%fused_computation.36 | loop fusion | bytes 1236992
  74.0 1.1 %copy_dynamic-update-slice_fusion.5 = f32[300,32,128]{2,0,1:T(8,128)S(1)} fusion(f32[300,32,128]{2,0,1:T(8,128)S(1)} %constant_dynamic-update-slice_fusion.1, f32[300,4,128]{2,1,0:T(4,128)} %collective-permute-done.2), kind=kLoop, calls=%fused_computation.37 | loop fusion | bytes 1236992
  75.3 0.5 fusion.30
  75.8 2.2 %copy.23 = f32[300,16,128]{2,1,0:T(8,128)} copy(f32[300,16,128]{2,0,1:T(8,128)S(1)} %get-tuple-element.9) | data formatting | bytes 4915200
  78.0 13.6 %psum.23 = f32[300]{0:T(512)S(1)} all-reduce(f32[300]{0:T(512)S(1)} %get-tuple-element.8), channel_id=1, replica_groups=mesh['member'=4,'space'=8] {'space'}, use_global_device_ids=true, to_apply=%region_5.6 | all-reduce | flops 300 | bytes 2400 | tf_op jit(solution)/shard_map/psum | solution.py:76
  91.6 1.8 %select_divide_fusion = f32[300]{0:T(512)} fusion(f32[300]{0:T(512)S(1)} %psum.23, f32[]{:T(128)} %bitcast.18, f32[]{:T(128)} %bitcast.17), kind=kLoop, calls=%fused_computation.62 | loop fusion | flops 900 | bytes 2408 | tf_op jit(solution)/shard_map/div | solution.py:77
  (10 shorter events, 0.3 us)
Async XLA Ops:
  0.6 8.0 %copy-start = (bf16[300,16,128]{2,1,0:T(8,128)(2,1)S(1)}, bf16[300,16,128]{2,1,0:T(8,128)(2,1)}, u32[]{:S(2)}) copy-start(bf16[300,16,128]{2,1,0:T(8,128)(2,1)} %param.4) | copy-start | bytes 3686404
  0.6 40.7 %copy-start.1 = (s32[2,16,128]{2,1,0:T(8,128)S(1)}, s32[2,16,128]{2,1,0:T(8,128)}, u32[]{:S(2)}) copy-start(s32[2,16,128]{2,1,0:T(8,128)} %param.5) | copy-start | bytes 49156
  3.4 20.9 %all-to-all-start = ((bf16[1,300,16,128]{3,1,0,2:T(8,128)(2,1)}), bf16[1,300,16,128]{3,1,0,2:T(8,128)(2,1)S(1)}, u32[]{:S(2)}, u32[]{:S(2)}) async-start(bf16[1,300,16,128]{3,1,0,2:T(8,128)(2,1)} %copy.11), calls=%async_computation | async-start | bytes 2490368 | tf_op jit(solution)/shard_map/all_to_all | solution.py:54
  25.3 15.8 %collective-permute-start = (f32[300,4,128]{2,1,0:T(4,128)S(1)}, f32[300,4,128]{2,1,0:T(4,128)S(1)}, u32[]{:S(2)}, u32[]{:S(2)}) collective-permute-start(f32[300,4,128]{2,1,0:T(4,128)S(1)} %copy.16), channel_id=1, source_target_pairs={{0,8},{8,16},{16,24},{24,0},{1,9},{9,17},{17,25},{25,1},{2,10},{10... | collective-permute-start | bytes 1843208 | tf_op jit(solution)/shard_map/ppermute | solution.py:20
  41.1 14.9 %collective-permute-start.1 = (f32[300,4,128]{2,1,0:T(4,128)S(1)}, f32[300,4,128]{2,1,0:T(4,128)S(1)}, u32[]{:S(2)}, u32[]{:S(2)}) collective-permute-start(f32[300,4,128]{2,1,0:T(4,128)S(1)} %collective-permute-done), channel_id=1, source_target_pairs={{0,8},{8,16},{16,24},{24,0},{1,9},{9,17},{17,25},{25,1},{2,10},{10... | collective-permute-start | bytes 1843208 | tf_op jit(solution)/shard_map/ppermute | solution.py:20
  56.0 16.8 %collective-permute-start.2 = (f32[300,4,128]{2,1,0:T(4,128)S(1)}, f32[300,4,128]{2,1,0:T(4,128)}, u32[]{:S(2)}, u32[]{:S(2)}) collective-permute-start(f32[300,4,128]{2,1,0:T(4,128)S(1)} %collective-permute-done.1), channel_id=1, source_target_pairs={{0,8},{8,16},{16,24},{24,0},{1,9},{9,17},{17,25},{25,1},{2,10},{10... | collective-permute-start | bytes 1843208 | tf_op jit(solution)/shard_map/ppermute | solution.py:20
